TPU v7x, 256 devices: a whole 4x4x8 slice. The times are simulated.
256 devices in a mesh: kpt: 4 (over y_lo, core), row: 8 (over z), col: 8 (over y_hi, x).
Axes of the slice: x: 4, y: 4 (y_hi: 2, y_lo: 2; y = y_hi * 2 + y_lo), z: 8, core: 2. Of those that a mesh axis runs over, the one named last changes fastest.
Arguments:
- a_matrix: bfloat16 [8, 4096, 4096], P('kpt', 'row', 'col'), parts along dimension 0, may hold values from -6 to 6
- b_matrix: bfloat16 [8, 4096, 4096], P('kpt', 'row', 'col'), parts along dimension 0, may hold values from -0.09375 to 0.09375
- a_level: int32 [128, 32], P('kpt'), parts along dimension 0, may hold values from 0 to 4, as said below
- b_level: int32 [128, 32], P('kpt'), parts along dimension 0, may hold values from 0 to 4, as said below
- limit: int32 [128, 32], P(('kpt', 'row'), 'col'), parts along dimension 0, may hold values from 3 to 8
Outputs:
- product: bfloat16 [8, 4096, 4096], P('kpt', 'row', 'col'), parts along dimension 0
- kept_count: int32 [128, 32], P(('kpt', 'row'), 'col'), parts along dimension 0
- kept_total: int32 [4], P('kpt'), parts along dimension 0
There are 4 independent parts, one for each index of `kpt`. A program takes and returns all parts, laid end to end along the dimension named above; each array names one. Nothing has to cross between parts.
Inputs may be any that keep to these rules, and one draw needn't show every extreme that they name: Each block's level is 0 (empty) or its norm exponent 1 to 4; the share of occupied blocks rises from some a sixth in the first block row of a_level (block column of b_level) to some six in seven in the last. `b_level`: as for a_level, with the share rising along block columns.
All inputs are finite; a program needn't handle non-finite values.
Results may differ from a plain program's by a relative error of at most 0.001.
Values may be sent and summed in bfloat16 or wider, within the bound.
A program may use at most 128 MiB of HBM per device.

v0:
```python
import jax
import jax.numpy as jnp
from jax import lax
from jax.sharding import Mesh
from jax.sharding import PartitionSpec as P

BLK = 128
COL = ("col_0", "col_1")
ROW_COL = ("row", "col_0", "col_1")


def joined_along(blocks, dim):
    dims = list(blocks.shape[1:])
    dims[dim] *= blocks.shape[0]
    return jnp.moveaxis(blocks, 0, dim).reshape(dims)


def stacked_from(shard, axes, turns):
    blocks = shard
    for k in turns:
        blocks = lax.all_gather(blocks, axes[k])
    done = turns[::-1]
    back = [done.index(k) for k in range(len(axes))]
    blocks = blocks.transpose(*back, *range(len(axes), blocks.ndim))
    return blocks.reshape(-1, *shard.shape)


def gathered_by_axis(shard, axes, turns, dim):
    return joined_along(stacked_from(shard, axes, turns), dim)


def from_everyone(shard, axis):
    count = lax.axis_size(axis)
    return lax.all_to_all(
        jnp.broadcast_to(shard[None], (count, *shard.shape)), axis, 0, 0, tiled=True
    )


def taken_together(shard, axis):
    return from_everyone(shard, axis).sum(axis=0)


def level_scale(levels):
    power = jnp.power(jnp.float32(2.0), (1 - levels).astype(jnp.float32))
    return jnp.where(levels > 0, power, jnp.float32(0.0))


def spread_blocks(small):
    return jnp.repeat(jnp.repeat(small, BLK, axis=0), BLK, axis=1)


def block_terms(a_piece, a_lev, b_piece, b_lev, limit):
    keep = (
        (a_lev[:, :, None] > 0)
        & (b_lev[None, :, :] > 0)
        & (a_lev[:, :, None] + b_lev[None, :, :] <= limit[:, None, :])
    )
    counted = jnp.sum(keep.astype(jnp.int32), axis=1)
    results = []
    for column in range(limit.shape[1]):
        mask = jnp.repeat(keep[:, :, column], BLK, axis=0)
        masked = jnp.where(mask[None], a_piece, jnp.zeros((), jnp.bfloat16))
        right = b_piece[:, :, column * BLK : (column + 1) * BLK]
        real_real = jnp.dot(masked[0], right[0], preferred_element_type=jnp.float32)
        imag_imag = jnp.dot(masked[1], right[1], preferred_element_type=jnp.float32)
        real_imag = jnp.dot(masked[0], right[1], preferred_element_type=jnp.float32)
        imag_real = jnp.dot(masked[1], right[0], preferred_element_type=jnp.float32)
        results.append(jnp.stack([real_real - imag_imag, real_imag + imag_real]))
    return (jnp.concatenate(results, axis=2), counted)


def shards(a_matrix, b_matrix, a_level, b_level, limit):
    row_place = lax.axis_index("row")
    col_place = lax.axis_index(COL)
    row_blocks = a_matrix.shape[1] // BLK
    col_blocks = a_matrix.shape[2] // BLK
    a_own = lax.dynamic_slice(
        a_level, (row_place * row_blocks, col_place * col_blocks), (row_blocks, col_blocks)
    )
    b_own = lax.dynamic_slice(
        b_level, (row_place * row_blocks, col_place * col_blocks), (row_blocks, col_blocks)
    )
    a_eff = a_matrix * spread_blocks(level_scale(a_own)).astype(jnp.bfloat16)[None]
    b_eff = b_matrix * spread_blocks(level_scale(b_own)).astype(jnp.bfloat16)[None]
    a_band = lax.dynamic_slice_in_dim(a_level, row_place * row_blocks, row_blocks, 0)
    b_band = lax.dynamic_slice_in_dim(b_level, col_place * col_blocks, col_blocks, 1)
    a_levels = jnp.repeat(a_band, BLK, axis=1)
    b_levels = jnp.repeat(b_band, BLK, axis=0)
    b_whole = lax.all_gather(b_eff, "row", axis=1, tiled=True)
    added, counted = block_terms(
        gathered_by_axis(a_eff, COL, (0, 1), 2), a_levels, b_whole, b_levels, limit
    )
    kept_count = counted // BLK
    kept_total = taken_together(jnp.sum(kept_count).reshape(1), ROW_COL)
    return (added.astype(jnp.bfloat16), kept_count, kept_total)


def solution(mesh):
    split = Mesh(
        mesh.devices.reshape(mesh.shape["kpt"], mesh.shape["row"], 2, 4),
        ("kpt", "row", "col_0", "col_1"),
    )
    placed = (
        P("kpt", "row", COL),
        P("kpt", "row", COL),
        P("kpt", None),
        P("kpt", None),
        P(("kpt", "row"), COL),
    )
    return jax.shard_map(
        shards,
        mesh=split,
        in_specs=placed,
        out_specs=(P("kpt", "row", COL), P(("kpt", "row"), COL), P("kpt")),
        check_vma=False,
    )
```

profile of v0, /device:TPU:28, one launch (start us, length us, event | category | flops | bytes accessed | tf_op | source)
XLA Modules:
  0.0 271.3 jit_solution(18135419596810637559)
XLA Ops:
  7.3 0.8 dynamic_slice.14
  9.0 2.3 broadcast_multiply_fusion.1
  11.4 40.9 %all-gather.8.cloned.1.call-done = bf16[4,512,512]{2,1,0:T(8,128)(2,1)} async-done(((bf16[2,512,512]{2,1,0:T(8,128)(2,1)}), bf16[4,512,512]{2,1,0:T(8,128)(2,1)}) %all-gather.8.cloned.1.call-update) | async-done | bytes 2097168 | tf_op jit(solution)/shard_map/all_gather | solution.py:21
  54.1 1.1 broadcast_multiply_fusion
  57.6 1.3 broadcast_in_dim.101
  58.8 12.9 %all-to-all-start = ((s32[64,1,1]{2,1,0:T(1,128)}), s32[64,1,1]{2,1,0:T(1,128)S(1)}, u32[]{:S(2)}, u32[]{:S(2)}) async-start(s32[64,1,1]{2,1,0:T(1,128)} %broadcast_in_dim.101), calls=%async_computation | async-start | bytes 65536 | tf_op jit(solution)/shard_map/all_to_all | solution.py:34
  71.9 0.8 copy.60
  72.7 12.2 %broadcast_in_dim.98 = pred[4,128,4096]{1,0,2:T(4,128)(4,1)S(1)} broadcast(pred[4,4096]{0,1:T(8,128)(4,1)S(1)} %copy.60), dimensions={0,2} | broadcast | bytes 2113536 | tf_op jit(solution)/shard_map/broadcast_in_dim | solution.py:61
  84.9 1.0 copy.87
  85.9 0.8 copy.59
  86.8 12.2 %broadcast_in_dim.95 = pred[4,128,4096]{1,0,2:T(4,128)(4,1)S(1)} broadcast(pred[4,4096]{0,1:T(8,128)(4,1)S(1)} %copy.59), dimensions={0,2} | broadcast | bytes 2113536 | tf_op jit(solution)/shard_map/broadcast_in_dim | solution.py:61
  99.0 2.3 copy.88
  101.3 0.8 copy.58
  102.1 12.2 %broadcast_in_dim.92 = pred[4,128,4096]{1,0,2:T(4,128)(4,1)S(1)} broadcast(pred[4,4096]{0,1:T(8,128)(4,1)S(1)} %copy.58), dimensions={0,2} | broadcast | bytes 2113536 | tf_op jit(solution)/shard_map/broadcast_in_dim | solution.py:61
  114.3 2.4 copy.89
  116.7 0.8 copy.51
  117.5 12.2 %broadcast_in_dim.83 = pred[4,128,4096]{1,0,2:T(4,128)(4,1)S(1)} broadcast(pred[4,4096]{0,1:T(8,128)(4,1)S(1)} %copy.51), dimensions={0,2} | broadcast | bytes 2113536 | tf_op jit(solution)/shard_map/broadcast_in_dim | solution.py:61
  129.7 2.3 copy.90
  133.4 7.4 %all-gather.10.cloned.1.call-done = bf16[8,2,512,512]{3,2,1,0:T(8,128)(2,1)} async-done(((bf16[2,2,512,512]{3,2,1,0:T(8,128)(2,1)}), bf16[8,2,512,512]{3,2,1,0:T(8,128)(2,1)}) %all-gather.10.cloned.1.call-update) | async-done | bytes 8388624 | tf_op jit(solution)/shard_map/all_gather | solution.py:21
  140.8 7.4 %copy.54 = bf16[2,4,2,512,512]{4,3,2,1,0:T(8,128)(2,1)} copy(bf16[2,4,2,512,512]{4,3,2,0,1:T(8,128)(2,1)} %bitcast.206) | data formatting | bytes 16777216 | tf_op jit(solution)/shard_map/transpose | solution.py:24
  148.2 11.9 %copy.55 = bf16[2,512,8,512]{1,3,2,0:T(8,128)(2,1)} copy(bf16[2,512,8,512]{3,1,0,2:T(8,128)(2,1)} %bitcast.197) | data formatting | bytes 16777216 | tf_op jit(solution)/shard_map/transpose | solution.py:15
  160.1 16.5 %bitcast_select_fusion.3 = (bf16[2,512,4096]{1,2,0:T(8,128)(2,1)}, bf16[2,512,4096]{1,2,0:T(8,128)(2,1)}, bf16[2,512,4096]{1,2,0:T(8,128)(2,1)}, bf16[2,512,4096]{1,2,0:T(8,128)(2,1)}) fusion(bf16[2,512,8,512]{1,3,2,0:T(8,128)(2,1)} %copy.55, pred[512,4096]{0,1:T(8,128)(4,1)} %bitcast.201, pred[512,4096]{0,1:T(8,128)(4,1)} %bitcast.200, ...), kind=kLoop, calls=%fused_computation.3 | loop fusion | flops 16777216 | bytes 50331648 | tf_op jit(solution)/shard_map/jit(_where)/select_n | solution.py:62
  176.6 61.8 %all-gather.6.cloned.1.call-done = bf16[2,4096,512]{2,1,0:T(8,128)(2,1)} async-done(((bf16[2,512,512]{2,1,0:T(8,128)(2,1)}), bf16[2,4096,512]{2,1,0:T(8,128)(2,1)}) %all-gather.6.cloned.1.call-update) | async-done | bytes 8388624 | tf_op jit(solution)/shard_map/all_gather | solution.py:89
  238.4 3.4 %fusion.1 = f32[512,128]{0,1:T(8,128)S(1)} fusion(bf16[2,512,4096]{1,2,0:T(8,128)(2,1)} %get-tuple-element.25, bf16[2,4096,512]{2,1,0:T(8,128)(2,1)} %all-gather.6.cloned.1.call-done), kind=kOutput, calls=%fused_computation.17 | convolution fusion | flops 536870912 | bytes 5505024 | tf_op jit(solution)/shard_map/dot_general | solution.py:64
  241.9 1.5 copy-done
  243.4 2.2 fusion
  246.4 2.8 %fusion.5 = f32[512,128]{0,1:T(8,128)S(1)} fusion(bf16[2,512,4096]{1,2,0:T(8,128)(2,1)S(1)} %bitcast.212, bf16[2,4096,512]{2,1,0:T(8,128)(2,1)} %all-gather.6.cloned.1.call-done), kind=kOutput, calls=%fused_computation.21 | convolution fusion | flops 536870912 | bytes 5505024 | tf_op jit(solution)/shard_map/dot_general | solution.py:64
  250.3 1.3 slice-done.3
  253.8 1.5 slice-done.1
  259.3 0.8 fusion.37
  260.1 0.8 fusion.34
  263.4 1.3 copy.62
  (68 shorter events, 17.0 us)
Async XLA Ops:
  7.2 48.1 %copy-start.2 = (s32[32,32]{1,0:T(8,128)S(1)}, s32[32,32]{1,0:T(8,128)}, u32[]{:S(2)}) copy-start(s32[32,32]{1,0:T(8,128)} %param.8) | copy-start | bytes 12292
  7.2 46.9 %copy-start.1 = (bf16[2,512,512]{2,1,0:T(8,128)(2,1)S(1)}, bf16[2,512,512]{2,1,0:T(8,128)(2,1)}, u32[]{:S(2)}) copy-start(bf16[2,512,512]{2,1,0:T(8,128)(2,1)} %param.6) | copy-start | bytes 3145732
  7.2 48.2 %copy-start.3 = (s32[4,4]{1,0:T(4,128)S(1)}, s32[4,4]{1,0:T(4,128)}, u32[]{:S(2)}) copy-start(s32[4,4]{1,0:T(4,128)} %param.9) | copy-start | bytes 196
  7.2 45.1 %all-gather.8.cloned.1.call-start = ((), (), s32[]{:S(2)}) async-start(), calls=%async_computation.2 | async-start | bytes 3145728 | tf_op jit(solution)/shard_map/all_gather | solution.py:21
  11.4 129.4 %all-gather.10.cloned.1.call-start = ((), (), s32[]{:S(2)}) async-start(), calls=%async_computation.3 | async-start | bytes 10485760 | tf_op jit(solution)/shard_map/all_gather | solution.py:21
  52.3 186.1 %all-gather.6.cloned.1.call-start = ((), (), s32[]{:S(2)}) async-start(), calls=%async_computation.1 | async-start | bytes 9437184 | tf_op jit(solution)/shard_map/all_gather | solution.py:89
  58.8 73.8 %all-to-all-start = ((s32[64,1,1]{2,1,0:T(1,128)}), s32[64,1,1]{2,1,0:T(1,128)S(1)}, u32[]{:S(2)}, u32[]{:S(2)}) async-start(s32[64,1,1]{2,1,0:T(1,128)} %broadcast_in_dim.101), calls=%async_computation | async-start | bytes 65536 | tf_op jit(solution)/shard_map/all_to_all | solution.py:34
  238.4 5.0 %copy-start = (bf16[2,512,4096]{1,2,0:T(8,128)(2,1)S(1)}, bf16[2,512,4096]{1,2,0:T(8,128)(2,1)}, u32[]{:S(2)}) copy-start(bf16[2,512,4096]{1,2,0:T(8,128)(2,1)} %get-tuple-element.25) | copy-start | bytes 25165828
  238.4 7.2 %slice-start.4 = ((s8[8388608]{0:T(1024)(128)(4,1)}), s8[4194304]{0:T(1024)(128)(4,1)S(1)}, s32[]{:S(2)}) async-start(s8[8388608]{0:T(1024)(128)(4,1)} %bitcast.211), calls=%async_computation.8 | async-start | bytes 8388608
  243.4 3.0 %slice-start.5 = ((s8[8388608]{0:T(1024)(128)(4,1)}), s8[4194304]{0:T(1024)(128)(4,1)S(1)}, s32[]{:S(2)}) async-start(s8[8388608]{0:T(1024)(128)(4,1)} %bitcast.211), calls=%async_computation.9 | async-start | bytes 8388608
  243.4 5.8 %copy-start.4 = (bf16[2,4096,512]{2,1,0:T(8,128)(2,1)S(1)}, bf16[2,4096,512]{2,1,0:T(8,128)(2,1)}, u32[]{:S(2)}) copy-start(bf16[2,4096,512]{2,1,0:T(8,128)(2,1)} %all-gather.6.cloned.1.call-done) | copy-start | bytes 25165828
  246.4 3.9 %slice-start.2 = ((s8[8388608]{0:T(1024)(128)(4,1)}), s8[4194304]{0:T(1024)(128)(4,1)S(1)}, s32[]{:S(2)}) async-start(s8[8388608]{0:T(1024)(128)(4,1)} %bitcast.209), calls=%async_computation.6 | async-start | bytes 8388608
  249.2 2.4 slice-start.3
  251.6 2.2 slice-start
  252.4 2.9 %slice-start.1 = ((s8[8388608]{0:T(1024)(128)(4,1)}), s8[4194304]{0:T(1024)(128)(4,1)S(1)}, s32[]{:S(2)}) async-start(s8[8388608]{0:T(1024)(128)(4,1)} %bitcast.207), calls=%async_computation.5 | async-start | bytes 8388608
Sparse Core Ops, SparseCore 0:
  11.5 40.7 all-gather.7
  54.1 86.6 all-gather.9
  143.2 95.1 all-gather.5
where the time goes:
time: 273 us; the launch traced here: 271 us
  waiting for transfers between devices  110 us (40%)
  local copies, waits for them, and re-layouts  93.3 us (34%)
  other arithmetic  21.8 us (8%)
  matrix products  18.8 us (7%)
  between operations  14.1 us (5%)
  starting transfers between devices  13.1 us (5%)
    all_gather x1, waiting for transfers between devices, shards(): b_whole = lax.all_gather(b_eff, 'row', axis=1, tiled=True)  61.8 us
    broadcast_in_dim x4, local copies, waits for them, and re-layouts, block_terms(): mask = jnp.repeat(keep[:, :, column], BLK, axis=0)  48.7 us
    all_gather x2, waiting for transfers between devices, stacked_from(): blocks = lax.all_gather(blocks, axes[k])  48.3 us
    unnamed x35, local copies, waits for them, and re-layouts  16.6 us
    select_n x1, other arithmetic, block_terms(): masked = jnp.where(mask[None], a_piece, jnp.zeros((), jnp.bfloat16))  16.5 us
    all_to_all x1, starting transfers between devices, from_everyone(): lax.all_to_all(jnp.broadcast_to(shard[None], (count, *shard.shape)), axis...  12.9 us
    transpose x1, local copies, waits for them, and re-layouts, joined_along(): return jnp.moveaxis(blocks, 0, dim).reshape(dims)  11.9 us
    dot_general x4, matrix products, block_terms(): real_real = jnp.dot(masked[0], right[0], preferred_element_type=jnp.float32)  7.82 us
  transfers between devices with their start and end apart: 4, of which 3 were waited for; matrix products, arithmetic and copies ran while one was open for 38% of the time, Pallas kernels for 0%

commit v1 on v0

v1 whole, which is shorter than its diff:
```python
import functools

import jax
import jax.numpy as jnp
from jax import lax
from jax.experimental import pallas as pl
from jax.experimental.pallas import tpu as pltpu
from jax.sharding import PartitionSpec as P

BLK = 128
Z = 8
X = 4
PIECES = 4
Z_STREAM = 14
X_STREAM = 12
MESH = pl.DeviceIdType.MESH


def piece(ref, slot, q):
    return ref.at[slot, :, pl.ds(pl.multiple_of(q * BLK, BLK), BLK), :]


def kernel(
    a_lev, b_lev, lim, a_hbm, b_hbm,
    out, cnt_out, tot_out,
    a_buf, b_buf, acc, scale, own_cnt, row_cnt, sum_cnt, col_cnt,
    in_sem, zr_send, zr_recv, zl_send, zl_recv,
    xr_send, xr_recv, xl_send, xl_recv, y_send, y_recv,
    rc_send, rc_recv, cc_send, cc_recv,
):
    z = lax.axis_index("row")
    c = lax.axis_index("col")
    x = c % X
    yh = c // X
    z_right, z_left = (z + 1) % Z, (z + Z - 1) % Z

    def col_at(dx, dy):
        return ((yh + dy) % 2) * X + (x + dx + X) % X

    x_right, x_left, y_far = col_at(1, 0), col_at(-1, 0), col_at(0, 1)

    a_in = pltpu.make_async_copy(a_hbm, a_buf.at[c], in_sem.at[0])
    b_in = pltpu.make_async_copy(b_hbm, b_buf.at[z], in_sem.at[1])
    b_in.start()
    a_in.start()

    barrier = pltpu.get_barrier_semaphore()
    for there in (z_right, z_left):
        pl.semaphore_signal(barrier, inc=1, device_id={"row": there}, device_id_type=MESH)
    for there in (x_right, x_left, y_far):
        pl.semaphore_signal(barrier, inc=1, device_id={"col": there}, device_id_type=MESH)
    pl.semaphore_wait(barrier, 5)
    b_in.wait()
    a_in.wait()

    def z_copy(right, t, sending):
        whole = t < 12
        far = jnp.where(whole, t // PIECES, 3)
        if right:
            q = jnp.where(whole, t % PIECES, t - 12)
            origin = (z - far - (0 if sending else 1) + 2 * Z) % Z
            sems = (zr_send.at[t], zr_recv.at[t])
            there = z_right
        else:
            q = jnp.where(whole, t % PIECES, t - 10)
            origin = (z + far + (0 if sending else 1)) % Z
            sems = (zl_send.at[t], zl_recv.at[t])
            there = z_left
        part = piece(b_buf, origin, q)
        return pltpu.make_async_remote_copy(
            part, part, *sems, device_id={"row": there}, device_id_type=MESH
        )

    def x_copy(right, u, sending):
        second = u >= 6
        v = jnp.where(second, u - 6, u)
        relayed = v >= 4
        dx = jnp.where(relayed, 1, 0) + (0 if sending else 1)
        dy = jnp.where(second, 1, 0)
        if right:
            q = jnp.where(relayed, v - 4, v)
            sems = (xr_send.at[u], xr_recv.at[u])
            origin, there = col_at(-dx, dy), x_right
        else:
            q = jnp.where(relayed, v - 2, v)
            sems = (xl_send.at[u], xl_recv.at[u])
            origin, there = col_at(dx, dy), x_left
        part = piece(a_buf, origin, q)
        return pltpu.make_async_remote_copy(
            part, part, *sems, device_id={"col": there}, device_id_type=MESH
        )

    def y_copy(v, sending):
        part = piece(a_buf, c if sending else y_far, v)
        return pltpu.make_async_remote_copy(
            part, part, y_send.at[v], y_recv.at[v], device_id={"col": y_far}, device_id_type=MESH
        )

    def count_to_row(d):
        return pltpu.make_async_remote_copy(
            own_cnt, row_cnt.at[d - 1], rc_send.at[d - 1], rc_recv.at[d - 1],
            device_id={"col": (c + d) % 8}, device_id_type=MESH,
        )

    def count_to_col(d):
        return pltpu.make_async_remote_copy(
            sum_cnt, col_cnt.at[d - 1], cc_send.at[d - 1], cc_recv.at[d - 1],
            device_id={"row": (z + d) % Z}, device_id_type=MESH,
        )

    def z_send(t):
        z_copy(True, t, True).start()
        z_copy(False, t, True).start()

    def x_send(u):
        x_copy(True, u, True).start()
        x_copy(False, u, True).start()

    z_send(0)
    x_send(0)
    y_copy(0, True).start()
    z_send(1)
    x_send(1)
    for v in range(1, PIECES):
        y_copy(v, True).start()

    def tabulate(k, counts):
        new = []
        for i in range(4):
            a = a_lev[4 * z + i, k]
            for j in range(4):
                b = b_lev[k, 4 * c + j]
                keep = (a > 0) & (b > 0) & (a + b <= lim[i, j])
                near = jnp.where(a + b >= 6, 4, a + b - 2)
                power = jnp.where(
                    a + b <= 4,
                    jnp.where(a + b <= 2, 1.0, jnp.where(a + b <= 3, 0.5, 0.25)),
                    jnp.where(
                        a + b <= 6,
                        jnp.where(a + b <= 5, 0.125, 0.0625),
                        jnp.where(a + b <= 7, 0.03125, 0.015625),
                    ),
                )
                scale[k, i * 4 + j] = jnp.where(keep, power, 0.0).astype(jnp.float32)
                new.append(counts[i * 4 + j] + jnp.where(keep, 1, 0))
        return tuple(new)

    counts = lax.fori_loop(0, 32, tabulate, (jnp.int32(0),) * 16)
    total = jnp.int32(0)
    for i in range(4):
        for j in range(4):
            cnt_out[i, j] = counts[i * 4 + j]
            total = total + counts[i * 4 + j]
    own_cnt[...] = jnp.full(own_cnt.shape, total, jnp.int32)
    acc[...] = jnp.zeros_like(acc)

    def multiply(m, q):
        k = 4 * m + q
        lane = pl.ds(pl.multiple_of(q * BLK, BLK), BLK)

        def one_column(j, _):
            cols = pl.ds(pl.multiple_of(j * BLK, BLK), BLK)
            b_re = b_buf[m, 0, lane, cols]
            b_im = b_buf[m, 1, lane, cols]
            right = jnp.concatenate(
                [jnp.concatenate([b_re, b_im], 1), jnp.concatenate([-b_im, b_re], 1)], 0
            )
            lefts = []
            for i in range(4):
                rows = pl.ds(i * BLK, BLK)
                by = scale[k, i * 4 + j].astype(jnp.bfloat16)
                lefts.append(
                    jnp.concatenate([a_buf[m, 0, rows, lane], a_buf[m, 1, rows, lane]], 1) * by
                )
            left = jnp.concatenate(lefts, 0)
            acc[j] += jnp.dot(left, right, preferred_element_type=jnp.float32)
            return 0

        lax.fori_loop(0, 4, one_column, 0)

    def a_slot_time(m):
        dx = (m % X - x + X) % X
        dy = jnp.where(m // X == yh, 0, 1)
        same = jnp.where(dx == 0, 0, jnp.where(dx == 2, 5, 3))
        other = jnp.where(dx == 0, 9, jnp.where(dx == 2, 13, 11))
        return jnp.where(dy == 0, same, other)

    def b_slot_time(m, q):
        d = (m - z + Z) % Z
        near = jnp.minimum(d, Z - d)
        return jnp.where(near == 0, 0, jnp.where(near == 4, 12 + q % 2, 4 * near - 4 + q))

    def x_step(slot):
        for u, at in enumerate((0, 1, 2, 3, 4, 5, 7, 8, 9, 11, 12, 13)):
            @pl.when(slot == at)
            def _():
                x_copy(True, u, False).wait_recv()
                x_copy(False, u, False).wait_recv()

        for v, at in enumerate((4, 6, 7, 9)):
            @pl.when(slot == at)
            def _():
                y_copy(v, False).wait_recv()

        for u, at in ((2, 0), (3, 1), (4, 2), (5, 3), (6, 4), (7, 6), (8, 7), (9, 9), (10, 9), (11, 11)):
            @pl.when(slot == at)
            def _():
                x_send(jnp.int32(u))

    def slot_body(slot, _):
        z_copy(True, slot, False).wait_recv()
        z_copy(False, slot, False).wait_recv()

        @pl.when(slot < Z_STREAM - 2)
        def _():
            z_send(slot + 2)

        x_step(slot)

        @pl.when(slot == 5)
        def _():
            for d in range(1, 8):
                count_to_row(d).start()

        @pl.when(slot == 8)
        def _():
            for d in range(1, 8):
                count_to_row(d).wait_recv()
            sum_cnt[...] = own_cnt[...] + jnp.sum(row_cnt[...], axis=0)

        @pl.when(slot == 9)
        def _():
            for d in range(1, 8):
                count_to_col(d).start()

        @pl.when(slot == 12)
        def _():
            for d in range(1, 8):
                count_to_col(d).wait_recv()
            everyone = sum_cnt[...] + jnp.sum(col_cnt[...], axis=0)
            tot_out[0] = everyone[0, 0]

        def one_source(m, _):
            a_at = a_slot_time(m)

            def one_piece(q, _):
                @pl.when(jnp.maximum(a_at, b_slot_time(m, q)) == slot)
                def _():
                    multiply(m, q)

                return 0

            @pl.when(a_at <= slot)
            def _():
                lax.fori_loop(0, PIECES, one_piece, 0)

            return 0

        lax.fori_loop(0, Z, one_source, 0)
        return 0

    lax.fori_loop(0, Z_STREAM, slot_body, 0)

    for j in range(4):
        for p in range(2):
            out[p, :, j * BLK : (j + 1) * BLK] = acc[j, :, p * BLK : (p + 1) * BLK].astype(
                jnp.bfloat16
            )

    def z_done(t, _):
        z_copy(True, t, True).wait_send()
        z_copy(False, t, True).wait_send()
        return 0

    def x_done(u, _):
        x_copy(True, u, True).wait_send()
        x_copy(False, u, True).wait_send()
        return 0

    def y_done(v, _):
        y_copy(v, True).wait_send()
        return 0

    lax.fori_loop(0, Z_STREAM, z_done, 0)
    lax.fori_loop(0, X_STREAM, x_done, 0)
    lax.fori_loop(0, PIECES, y_done, 0)
    for d in range(1, 8):
        count_to_row(d).wait_send()
        count_to_col(d).wait_send()


def shards(a_matrix, b_matrix, a_level, b_level, limit):
    parts, rows, columns = a_matrix.shape
    dma = pltpu.SemaphoreType.DMA
    smem = pl.BlockSpec(memory_space=pltpu.SMEM)
    hbm = pl.BlockSpec(memory_space=pl.ANY)
    return pl.pallas_call(
        kernel,
        out_shape=(
            jax.ShapeDtypeStruct((parts, rows, columns), jnp.bfloat16),
            jax.ShapeDtypeStruct((4, 4), jnp.int32),
            jax.ShapeDtypeStruct((1,), jnp.int32),
        ),
        in_specs=[smem, smem, smem, hbm, hbm],
        out_specs=(pl.BlockSpec(memory_space=pltpu.VMEM), smem, smem),
        scratch_shapes=[
            pltpu.VMEM((8, parts, rows, columns), jnp.bfloat16),
            pltpu.VMEM((Z, parts, rows, columns), jnp.bfloat16),
            pltpu.VMEM((4, rows, 2 * BLK), jnp.float32),
            pltpu.SMEM((32, 16), jnp.float32),
            pltpu.VMEM((8, BLK), jnp.int32),
            pltpu.VMEM((7, 8, BLK), jnp.int32),
            pltpu.VMEM((8, BLK), jnp.int32),
            pltpu.VMEM((7, 8, BLK), jnp.int32),
            dma((2,)),
            dma((Z_STREAM,)), dma((Z_STREAM,)), dma((Z_STREAM,)), dma((Z_STREAM,)),
            dma((X_STREAM,)), dma((X_STREAM,)), dma((X_STREAM,)), dma((X_STREAM,)),
            dma((PIECES,)), dma((PIECES,)),
            dma((7,)), dma((7,)), dma((7,)), dma((7,)),
        ],
        compiler_params=pltpu.CompilerParams(
            collective_id=0, has_side_effects=True, vmem_limit_bytes=40 * 1024 * 1024
        ),
        cost_estimate=pl.CostEstimate(
            flops=8 * rows * 4096 * columns, bytes_accessed=6 << 20, transcendentals=0
        ),
    )(a_level, b_level, limit, a_matrix, b_matrix)


def solution(mesh):
    placed = (
        P("kpt", "row", "col"),
        P("kpt", "row", "col"),
        P("kpt", None),
        P("kpt", None),
        P(("kpt", "row"), "col"),
    )
    return jax.shard_map(
        shards,
        mesh=mesh,
        in_specs=placed,
        out_specs=(P("kpt", "row", "col"), P(("kpt", "row"), "col"), P("kpt")),
        check_vma=False,
    )
```

time: 273 us -> 109 us (0.40)
  waiting for transfers between devices: 110 us -> 0 us
  Pallas kernels: 0 us -> 98.9 us
  local copies, waits for them, and re-layouts: 93.3 us -> 6.11 us
  other arithmetic: 21.8 us -> 0 us
  matrix products: 18.8 us -> 0 us
  starting transfers between devices: 13.1 us -> 0 us
  between operations: 14.1 us -> 2.34 us
    all_gather x3 -> x0, waiting for transfers between devices: 110 us -> none  [the longest x1 61.8 us: shards(): b_whole = lax.all_gather(b_eff, 'row', axis=1, tiled=True)]
    pallas_call x0 -> x1, Pallas kernels: none -> 98.9 us  [shards(): pl.pallas_call(kernel, out_shape=(jax.ShapeDtypeStruct((parts, rows, colu...]
    broadcast_in_dim x9 -> x0, local copies, waits for them, and re-layouts: 51.2 us -> none  [the longest x4 48.7 us: block_terms(): mask = jnp.repeat(keep[:, :, column], BLK, axis=0)]
    transpose x2 -> x0, local copies, waits for them, and re-layouts: 19.3 us -> none  [the longest x1 11.9 us: joined_along(): return jnp.moveaxis(blocks, 0, dim).reshape(dims)]
    dot_general x16 -> x0, matrix products: 18.8 us -> none  [the longest x4 7.82 us: block_terms(): real_real = jnp.dot(masked[0], right[0], preferred_element_type=jnp.float32)]
    select_n x1 -> x0, other arithmetic: 16.5 us -> none  [block_terms(): masked = jnp.where(mask[None], a_piece, jnp.zeros((), jnp.bfloat16))]
    all_to_all x1 -> x0, starting transfers between devices: 12.9 us -> none  [from_everyone(): lax.all_to_all(jnp.broadcast_to(shard[None], (count, *shard.shape)), axis...]
    unnamed x35 -> x12, local copies, waits for them, and re-layouts: 16.6 us -> 6.11 us
  transfers between devices with their start and end apart: 4 -> 0, of which waited for: 3 -> 0; matrix products, arithmetic and copies ran while one was open for 38% -> 0% of each run, Pallas kernels for 0% -> 0%
where the time goes in v1:
time: 109 us; the launch traced here: 107 us
  Pallas kernels  98.9 us (91%)
  local copies, waits for them, and re-layouts  6.11 us (6%)
  between operations  2.34 us (2%)
    pallas_call x1, Pallas kernels, shards(): pl.pallas_call(kernel, out_shape=(jax.ShapeDtypeStruct((parts, rows, colu...  98.9 us
    unnamed x12, local copies, waits for them, and re-layouts  6.11 us

profile of v1, /device:TPU:28, one launch (start us, length us, event | category | flops | bytes accessed | tf_op | source)
XLA Modules:
  0.0 107.3 jit_solution(15486531790116565725)
XLA Ops:
  0.6 0.0 copy-start
  0.6 1.2 %copy-done = bf16[2,512,512]{2,1,0:T(8,128)(2,1)S(1)} copy-done((bf16[2,512,512]{2,1,0:T(8,128)(2,1)S(1)}, bf16[2,512,512]{2,1,0:T(8,128)(2,1)}, u32[]{:S(2)}) %copy-start) | copy-done | bytes 1048600
  1.9 0.0 copy-start.1
  1.9 1.2 %copy-done.1 = bf16[2,512,512]{2,1,0:T(8,128)(2,1)S(1)} copy-done((bf16[2,512,512]{2,1,0:T(8,128)(2,1)S(1)}, bf16[2,512,512]{2,1,0:T(8,128)(2,1)}, u32[]{:S(2)}) %copy-start.1) | copy-done | bytes 1048600
  3.1 0.0 copy-start.2
  3.1 0.7 copy-done.2
  3.8 0.0 copy-start.3
  3.8 0.7 copy-done.3
  4.5 0.0 copy-start.4
  4.5 0.7 copy-done.4
  5.2 98.9 %shard_map.76 = (bf16[2,512,512]{2,1,0:T(8,128)(2,1)S(1)}, s32[4,4]{1,0:T(4,128)S(1)}, s32[1]{0:T(128)}) custom-call(s32[32,32]{1,0:T(8,128)S(1)} %copy-done.2, s32[32,32]{1,0:T(8,128)S(1)} %copy-done.3, s32[4,4]{1,0:T(4,128)S(1)} %copy-done.4, bf16[2,512,512]{2,1,0:T(8,128)(2,1)S(1)} %copy-done, bf16[2,512,512]{2,1,0:T(8,128)(2,1)S(1)} %copy-done.1), custom_call_target="tpu_custom_call" | custom-call | flops 8589934592 | bytes 6291456 | tf_op jit(solution)/shard_map/pallas_call | solution.py:297
  104.1 1.0 copy.11
  105.0 0.6 copy.12
Async XLA Ops:
  0.6 1.2 %copy-start = (bf16[2,512,512]{2,1,0:T(8,128)(2,1)S(1)}, bf16[2,512,512]{2,1,0:T(8,128)(2,1)}, u32[]{:S(2)}) copy-start(bf16[2,512,512]{2,1,0:T(8,128)(2,1)} %a_hbm.1) | copy-start | bytes 3145732
  1.9 1.2 %copy-start.1 = (bf16[2,512,512]{2,1,0:T(8,128)(2,1)S(1)}, bf16[2,512,512]{2,1,0:T(8,128)(2,1)}, u32[]{:S(2)}) copy-start(bf16[2,512,512]{2,1,0:T(8,128)(2,1)} %b_hbm.1) | copy-start | bytes 3145732
  3.1 0.7 copy-start.2
  3.8 0.7 copy-start.3
  4.5 0.7 copy-start.4

commit v2 on v1

--- a/solution.py
+++ b/solution.py
@@ -21,10 +21,10 @@
 
 
 def kernel(
-    a_lev, b_lev, lim, a_hbm, b_hbm,
-    out, cnt_out, tot_out,
-    a_buf, b_buf, acc, scale, own_cnt, row_cnt, sum_cnt, col_cnt,
-    in_sem, zr_send, zr_recv, zl_send, zl_recv,
+    a_lev_hbm, b_lev_hbm, lim_hbm, a_hbm, b_hbm,
+    acc, cnt_out, tot_out,
+    a_lev, b_lev, lim, a_buf, b_buf, scale, own_cnt, row_cnt, sum_cnt, col_cnt,
+    lev_sem, in_sem, zr_send, zr_recv, zl_send, zl_recv,
     xr_send, xr_recv, xl_send, xl_recv, y_send, y_recv,
     rc_send, rc_recv, cc_send, cc_recv,
 ):
@@ -43,6 +43,14 @@
     b_in = pltpu.make_async_copy(b_hbm, b_buf.at[z], in_sem.at[1])
     b_in.start()
     a_in.start()
+    levels_in = [
+        pltpu.make_async_copy(there, here, lev_sem.at[n])
+        for n, (there, here) in enumerate(
+            ((a_lev_hbm, a_lev), (b_lev_hbm, b_lev), (lim_hbm, lim))
+        )
+    ]
+    for copy in levels_in:
+        copy.start()
 
     barrier = pltpu.get_barrier_semaphore()
     for there in (z_right, z_left):
@@ -131,7 +139,6 @@
             for j in range(4):
                 b = b_lev[k, 4 * c + j]
                 keep = (a > 0) & (b > 0) & (a + b <= lim[i, j])
-                near = jnp.where(a + b >= 6, 4, a + b - 2)
                 power = jnp.where(
                     a + b <= 4,
                     jnp.where(a + b <= 2, 1.0, jnp.where(a + b <= 3, 0.5, 0.25)),
@@ -145,6 +152,8 @@
                 new.append(counts[i * 4 + j] + jnp.where(keep, 1, 0))
         return tuple(new)
 
+    for copy in levels_in:
+        copy.wait()
     counts = lax.fori_loop(0, 32, tabulate, (jnp.int32(0),) * 16)
     total = jnp.int32(0)
     for i in range(4):
@@ -158,8 +167,8 @@
         k = 4 * m + q
         lane = pl.ds(pl.multiple_of(q * BLK, BLK), BLK)
 
-        def one_column(j, _):
-            cols = pl.ds(pl.multiple_of(j * BLK, BLK), BLK)
+        def one_column(j):
+            cols = pl.ds(j * BLK, BLK)
             b_re = b_buf[m, 0, lane, cols]
             b_im = b_buf[m, 1, lane, cols]
             right = jnp.concatenate(
@@ -173,16 +182,18 @@
                     jnp.concatenate([a_buf[m, 0, rows, lane], a_buf[m, 1, rows, lane]], 1) * by
                 )
             left = jnp.concatenate(lefts, 0)
-            acc[j] += jnp.dot(left, right, preferred_element_type=jnp.float32)
-            return 0
-
-        lax.fori_loop(0, 4, one_column, 0)
+            both = jnp.dot(left, right, preferred_element_type=jnp.float32)
+            acc[0, :, cols] += both[:, :BLK]
+            acc[1, :, cols] += both[:, BLK:]
+
+        for j in range(4):
+            one_column(j)
 
     def a_slot_time(m):
         dx = (m % X - x + X) % X
         dy = jnp.where(m // X == yh, 0, 1)
         same = jnp.where(dx == 0, 0, jnp.where(dx == 2, 5, 3))
-        other = jnp.where(dx == 0, 9, jnp.where(dx == 2, 13, 11))
+        other = jnp.where(dx == 0, 8, jnp.where(dx == 2, 12, 10))
         return jnp.where(dy == 0, same, other)
 
     def b_slot_time(m, q):
@@ -191,18 +202,18 @@
         return jnp.where(near == 0, 0, jnp.where(near == 4, 12 + q % 2, 4 * near - 4 + q))
 
     def x_step(slot):
-        for u, at in enumerate((0, 1, 2, 3, 4, 5, 7, 8, 9, 11, 12, 13)):
+        for u, at in enumerate((0, 1, 2, 3, 4, 5, 7, 8, 9, 10, 11, 12)):
             @pl.when(slot == at)
             def _():
                 x_copy(True, u, False).wait_recv()
                 x_copy(False, u, False).wait_recv()
 
-        for v, at in enumerate((4, 6, 7, 9)):
+        for v, at in enumerate((4, 5, 6, 8)):
             @pl.when(slot == at)
             def _():
                 y_copy(v, False).wait_recv()
 
-        for u, at in ((2, 0), (3, 1), (4, 2), (5, 3), (6, 4), (7, 6), (8, 7), (9, 9), (10, 9), (11, 11)):
+        for u, at in ((2, 0), (3, 1), (4, 2), (5, 3), (6, 4), (7, 5), (8, 6), (9, 8), (10, 9), (11, 10)):
             @pl.when(slot == at)
             def _():
                 x_send(jnp.int32(u))
@@ -260,12 +271,6 @@
         return 0
 
     lax.fori_loop(0, Z_STREAM, slot_body, 0)
-
-    for j in range(4):
-        for p in range(2):
-            out[p, :, j * BLK : (j + 1) * BLK] = acc[j, :, p * BLK : (p + 1) * BLK].astype(
-                jnp.bfloat16
-            )
 
     def z_done(t, _):
         z_copy(True, t, True).wait_send()
@@ -289,29 +294,49 @@
         count_to_col(d).wait_send()
 
 
+def round_kernel(acc, cnt, tot, out, cnt_out, tot_out, stage, sems):
+    def piece_out(i):
+        rows = pl.ds(i * BLK, BLK)
+        return pltpu.make_async_copy(stage.at[:, rows, :], out.at[:, rows, :], sems.at[i])
+
+    for i in range(4):
+        rows = slice(i * BLK, (i + 1) * BLK)
+        stage[:, rows, :] = acc[:, rows, :].astype(jnp.bfloat16)
+        piece_out(i).start()
+    for i in range(4):
+        for j in range(4):
+            cnt_out[i, j] = cnt[i, j]
+    tot_out[0] = tot[0]
+    for i in range(4):
+        piece_out(i).wait()
+
+
 def shards(a_matrix, b_matrix, a_level, b_level, limit):
     parts, rows, columns = a_matrix.shape
     dma = pltpu.SemaphoreType.DMA
     smem = pl.BlockSpec(memory_space=pltpu.SMEM)
-    hbm = pl.BlockSpec(memory_space=pl.ANY)
-    return pl.pallas_call(
+    hbm = pl.BlockSpec(memory_space=pltpu.HBM)
+    acc, cnt, tot = pl.pallas_call(
         kernel,
         out_shape=(
-            jax.ShapeDtypeStruct((parts, rows, columns), jnp.bfloat16),
-            jax.ShapeDtypeStruct((4, 4), jnp.int32),
-            jax.ShapeDtypeStruct((1,), jnp.int32),
+            pltpu.VMEM((parts, rows, columns), jnp.float32),
+            pltpu.SMEM((4, 4), jnp.int32),
+            pltpu.SMEM((1,), jnp.int32),
         ),
-        in_specs=[smem, smem, smem, hbm, hbm],
+        in_specs=[hbm] * 5,
         out_specs=(pl.BlockSpec(memory_space=pltpu.VMEM), smem, smem),
         scratch_shapes=[
+            pltpu.SMEM((32, 32), jnp.int32),
+            pltpu.SMEM((32, 32), jnp.int32),
+            pltpu.SMEM((4, 4), jnp.int32),
             pltpu.VMEM((8, parts, rows, columns), jnp.bfloat16),
             pltpu.VMEM((Z, parts, rows, columns), jnp.bfloat16),
-            pltpu.VMEM((4, rows, 2 * BLK), jnp.float32),
             pltpu.SMEM((32, 16), jnp.float32),
             pltpu.VMEM((8, BLK), jnp.int32),
             pltpu.VMEM((7, 8, BLK), jnp.int32),
             pltpu.VMEM((8, BLK), jnp.int32),
             pltpu.VMEM((7, 8, BLK), jnp.int32),
+            dma((3,)),
             dma((2,)),
             dma((Z_STREAM,)), dma((Z_STREAM,)), dma((Z_STREAM,)), dma((Z_STREAM,)),
             dma((X_STREAM,)), dma((X_STREAM,)), dma((X_STREAM,)), dma((X_STREAM,)),
@@ -319,12 +344,25 @@
             dma((7,)), dma((7,)), dma((7,)), dma((7,)),
         ],
         compiler_params=pltpu.CompilerParams(
-            collective_id=0, has_side_effects=True, vmem_limit_bytes=40 * 1024 * 1024
+            collective_id=0, has_side_effects=True, vmem_limit_bytes=61 << 20
         ),
         cost_estimate=pl.CostEstimate(
             flops=8 * rows * 4096 * columns, bytes_accessed=6 << 20, transcendentals=0
         ),
     )(a_level, b_level, limit, a_matrix, b_matrix)
+    vmem = pl.BlockSpec(memory_space=pltpu.VMEM)
+    return pl.pallas_call(
+        round_kernel,
+        out_shape=(
+            jax.ShapeDtypeStruct((parts, rows, columns), jnp.bfloat16),
+            jax.ShapeDtypeStruct((4, 4), jnp.int32),
+            jax.ShapeDtypeStruct((1,), jnp.int32),
+        ),
+        in_specs=[vmem, smem, smem],
+        out_specs=(hbm, smem, smem),
+        scratch_shapes=[pltpu.VMEM((parts, rows, columns), jnp.bfloat16), dma((4,))],
+        compiler_params=pltpu.CompilerParams(vmem_limit_bytes=48 << 20),
+    )(acc, cnt, tot)
 
 
 def solution(mesh):

time: 109 us -> 94.2 us (0.86)
  Pallas kernels: 98.9 us -> 92.1 us
  local copies, waits for them, and re-layouts: 6.11 us -> 0 us
  between operations: 2.34 us -> 0.64 us
    pallas_call x1 -> x2, Pallas kernels: 98.9 us -> 92.1 us  [the longest x1 90.5 us: shards(): pl.pallas_call(kernel, out_shape=(pltpu.VMEM((parts, rows, columns), jnp....]
    unnamed x12 -> x0, local copies, waits for them, and re-layouts: 6.11 us -> none
where the time goes in v2:
time: 94.2 us; the launch traced here: 92.7 us
  Pallas kernels  92.1 us (98%)
    pallas_call x1, Pallas kernels, shards(): pl.pallas_call(kernel, out_shape=(pltpu.VMEM((parts, rows, columns), jnp....  90.5 us

profile of v2, /device:TPU:28, one launch (start us, length us, event | category | flops | bytes accessed | tf_op | source)
XLA Modules:
  0.0 92.7 jit_solution(7601443142929135651)
XLA Ops:
  0.6 90.5 %shard_map.76 = (f32[2,512,512]{2,1,0:T(8,128)S(1)}, s32[4,4]{1,0:T(4,128)S(4)}, s32[1]{0:T(128)S(4)}) custom-call(s32[32,32]{1,0:T(8,128)} %a_lev_hbm.1, s32[32,32]{1,0:T(8,128)} %b_lev_hbm.1, s32[4,4]{1,0:T(4,128)} %lim_hbm.1, bf16[2,512,512]{2,1,0:T(8,128)(2,1)} %a_hbm.1, bf16[2,512,512]{2,1,0:T(8,128)(2,1)} %b_hbm.1), custom_call_target="tpu_custom_call" | custom-call | flops 8589934592 | bytes 6291456 | tf_op jit(solution)/shard_map/pallas_call | solution.py:319
  91.1 1.6 %shard_map.77 = (bf16[2,512,512]{2,1,0:T(8,128)(2,1)}, s32[4,4]{1,0:T(4,128)}, s32[1]{0:T(128)}) custom-call(f32[2,512,512]{2,1,0:T(8,128)S(1)} %get-tuple-element.6.acc, s32[4,4]{1,0:T(4,128)S(4)} %get-tuple-element.7.cnt, s32[1]{0:T(128)S(4)} %get-tuple-element.8.tot), custom_call_target="tpu_custom_call" | custom-call | tf_op jit(solution)/shard_map/pallas_call | solution.py:354

commit v3 on v2

v3 whole, which is shorter than its diff:
```python
import functools

import jax
import jax.numpy as jnp
from jax import lax
from jax.experimental import pallas as pl
from jax.experimental.pallas import tpu as pltpu
from jax.sharding import PartitionSpec as P

BLK = 128
Z = 8
X = 4
PIECES = 4
Z_STREAM = 14
X_STREAM = 12
DEPTH = 4
X_DEPTH = 3
MESH = pl.DeviceIdType.MESH


def piece(ref, slot, q):
    return ref.at[slot, :, pl.ds(pl.multiple_of(q * BLK, BLK), BLK), :]


def kernel(
    a_lev_hbm, b_lev_hbm, lim_hbm, a_hbm, b_hbm,
    acc, cnt_out, tot_out,
    a_lev, b_lev, lim, a_buf, b_buf, scale, power, own_cnt, row_cnt, sum_cnt, col_cnt,
    lev_sem, in_sem, zr_send, zr_recv, zl_send, zl_recv,
    xr_send, xr_recv, xl_send, xl_recv, y_send, y_recv,
    rc_send, rc_recv, cc_send, cc_recv,
    from_right, from_left, from_x_right, from_x_left, from_y, last_in,
):
    z = lax.axis_index("row")
    c = lax.axis_index("col")
    x = c % X
    yh = c // X
    z_right, z_left = (z + 1) % Z, (z + Z - 1) % Z

    def col_at(dx, dy):
        return ((yh + dy) % 2) * X + (x + dx + X) % X

    x_right, x_left, y_far = col_at(1, 0), col_at(-1, 0), col_at(0, 1)

    a_in, b_in = [], []
    for q in range(PIECES):
        rows = pl.ds(q * BLK, BLK)
        b_in.append(
            pltpu.make_async_copy(b_hbm.at[:, rows, :], piece(b_buf, z, q), in_sem.at[q])
        )
        a_in.append(
            pltpu.make_async_copy(a_hbm.at[:, rows, :], piece(a_buf, c, q), in_sem.at[PIECES + q])
        )
        b_in[q].start()
        a_in[q].start()
    levels_in = [
        pltpu.make_async_copy(there, here, lev_sem.at[n])
        for n, (there, here) in enumerate(
            ((a_lev_hbm, a_lev), (b_lev_hbm, b_lev), (lim_hbm, lim))
        )
    ]
    for copy in levels_in:
        copy.start()

    barrier = pltpu.get_barrier_semaphore()

    def signal(sem, **there):
        pl.semaphore_signal(sem, inc=1, device_id=there, device_id_type=MESH)

    def one_if(condition):
        return jnp.where(condition, 1, 0)

    @pl.when(z < Z - 1)
    def _():
        signal(barrier, row=z_right)

    @pl.when(z == 0)
    def _():
        signal(barrier, row=z_left)

    @pl.when(x < X - 1)
    def _():
        signal(barrier, col=x_right)

    @pl.when(x == 0)
    def _():
        signal(barrier, col=x_left)

    @pl.when(yh == 0)
    def _():
        signal(barrier, col=y_far)

    lower = one_if(z > 0) + one_if(z == Z - 1) + one_if(x > 0) + one_if(x == X - 1) + yh

    @pl.when(lower > 0)
    def _():
        pl.semaphore_wait(barrier, lower)


    def z_copy(right, t, sending):
        whole = t < 12
        far = jnp.where(whole, t // PIECES, 3)
        if right:
            q = jnp.where(whole, t % PIECES, t - 12)
            origin = (z - far - (0 if sending else 1) + 2 * Z) % Z
            sems = (zr_send.at[t], zr_recv.at[t])
            there = z_right
        else:
            q = PIECES - 1 - t % PIECES
            origin = (z + far + (0 if sending else 1)) % Z
            sems = (zl_send.at[t], zl_recv.at[t])
            there = z_left
        part = piece(b_buf, origin, q)
        return pltpu.make_async_remote_copy(
            part, part, *sems, device_id={"row": there}, device_id_type=MESH
        )

    def z_last(right, part, sending):
        q = 1 if right or part == 4 else 2
        far = 3 if sending else 4
        origin = (z - far + Z) % Z if right else (z + far) % Z
        sems = (zr_send, zr_recv) if right else (zl_send, zl_recv)
        quarter = 3 if part == 4 else part
        block = b_buf.at[origin, :, pl.ds(q * BLK, BLK), pl.ds(quarter * BLK, BLK)]
        return pltpu.make_async_remote_copy(
            block, block, sems[0].at[Z_STREAM - 1 + part], sems[1].at[Z_STREAM - 1 + part],
            device_id={"row": z_right if right else z_left}, device_id_type=MESH,
        )

    def x_copy(right, u, sending):
        second = u >= 6
        v = jnp.where(second, u - 6, u)
        relayed = v >= 4
        dx = jnp.where(relayed, 1, 0) + (0 if sending else 1)
        dy = jnp.where(second, 1, 0)
        if right:
            q = jnp.where(relayed, v - 4, v)
            sems = (xr_send.at[u], xr_recv.at[u])
            origin, there = col_at(-dx, dy), x_right
        else:
            q = jnp.where(relayed, v - 2, v)
            sems = (xl_send.at[u], xl_recv.at[u])
            origin, there = col_at(dx, dy), x_left
        part = piece(a_buf, origin, q)
        return pltpu.make_async_remote_copy(
            part, part, *sems, device_id={"col": there}, device_id_type=MESH
        )

    def y_copy(v, sending):
        part = piece(a_buf, c if sending else y_far, v)
        return pltpu.make_async_remote_copy(
            part, part, y_send.at[v], y_recv.at[v], device_id={"col": y_far}, device_id_type=MESH
        )

    def count_to_row(d):
        return pltpu.make_async_remote_copy(
            own_cnt, row_cnt.at[d - 1], rc_send.at[d - 1], rc_recv.at[d - 1],
            device_id={"col": (c + d) % 8}, device_id_type=MESH,
        )

    def count_to_col(d):
        return pltpu.make_async_remote_copy(
            sum_cnt, col_cnt.at[d - 1], cc_send.at[d - 1], cc_recv.at[d - 1],
            device_id={"row": (z + d) % Z}, device_id_type=MESH,
        )

    def z_send(t):
        z_copy(True, t, True).start()
        z_copy(False, t, True).start()

    def x_send(u):
        x_copy(True, u, True).start()
        x_copy(False, u, True).start()

    def first_z(right):
        for q in range(DEPTH):
            z_copy(right, jnp.int32(q), True).start()

    def first_x(right):
        for q in range(X_DEPTH):
            x_copy(right, jnp.int32(q), True).start()

    for q in range(DEPTH):
        b_in[q].wait()

    @pl.when(z == Z - 1)
    def _():
        first_z(True)
        signal(from_left, row=z_right)

    @pl.when(z > 0)
    def _():
        first_z(False)
        signal(from_right, row=z_left)

    @pl.when(x == X - 1)
    def _():
        signal(from_x_left, col=x_right)

    @pl.when(x > 0)
    def _():
        signal(from_x_right, col=x_left)

    @pl.when(yh == 1)
    def _():
        signal(from_y, col=y_far)

    @pl.when(z < Z - 1)
    def _():
        pl.semaphore_wait(from_right, 1)
        first_z(True)

    for q in range(PIECES):
        a_in[q].wait()

    @pl.when(x == X - 1)
    def _():
        first_x(True)

    @pl.when(x > 0)
    def _():
        first_x(False)

    @pl.when(yh == 0)
    def _():
        pl.semaphore_wait(from_y, 1)

    for q in range(PIECES):
        y_copy(q, True).start()

    @pl.when(x < X - 1)
    def _():
        pl.semaphore_wait(from_x_right, 1)
        first_x(True)

    @pl.when(x == 0)
    def _():
        pl.semaphore_wait(from_x_left, 1)
        first_x(False)

    @pl.when(z == 0)
    def _():
        pl.semaphore_wait(from_left, 1)
        first_z(False)
        signal(last_in, row=z_right)

    for s in range(33):
        power[s] = 2.0 ** (2 - s) if 2 <= s <= 8 else 0.0

    def tabulate(k, counts):
        new = []
        b_four = []
        for j in range(4):
            b = b_lev[k, 4 * c + j]
            b_four.append(jnp.where(b > 0, b, 16))
        for i in range(4):
            a = a_lev[4 * z + i, k]
            a = jnp.where(a > 0, a, 16)
            for j in range(4):
                both = a + b_four[j]
                keep = both <= lim[i, j]
                scale[k, i * 4 + j] = jnp.where(keep, power[both], 0.0)
                new.append(counts[i * 4 + j] + jnp.where(keep, 1, 0))
        return tuple(new)

    for copy in levels_in:
        copy.wait()
    counts = lax.fori_loop(0, 32, tabulate, (jnp.int32(0),) * 16)
    total = jnp.int32(0)
    for i in range(4):
        for j in range(4):
            cnt_out[i, j] = counts[i * 4 + j]
            total = total + counts[i * 4 + j]
    own_cnt[...] = jnp.full(own_cnt.shape, total, jnp.int32)
    acc[...] = jnp.zeros_like(acc)

    def multiply(m, pieces, columns=range(4)):
        for j in columns:
            cols = pl.ds(j * BLK, BLK)
            lefts, rights = [], []
            for q in pieces:
                lane = pl.ds(pl.multiple_of(q * BLK, BLK), BLK)
                b_re = b_buf[m, 0, lane, cols]
                b_im = b_buf[m, 1, lane, cols]
                rights += [jnp.concatenate([b_re, b_im], 1), jnp.concatenate([-b_im, b_re], 1)]
                bands = []
                for i in range(4):
                    rows = pl.ds(i * BLK, BLK)
                    by = scale[4 * m + q, i * 4 + j].astype(jnp.bfloat16)
                    bands.append(
                        jnp.concatenate([a_buf[m, 0, rows, lane], a_buf[m, 1, rows, lane]], 1) * by
                    )
                lefts.append(jnp.concatenate(bands, 0))
            both = jnp.dot(
                jnp.concatenate(lefts, 1),
                jnp.concatenate(rights, 0),
                preferred_element_type=jnp.float32,
            )
            acc[0, :, cols] += both[:, :BLK]
            acc[1, :, cols] += both[:, BLK:]

    def a_slot_time(m):
        dx = (m % X - x + X) % X
        dy = jnp.where(m // X == yh, 0, 1)
        same = jnp.where(dx == 0, 0, jnp.where(dx == 2, 5, 3))
        other = jnp.where(dx == 0, 8, jnp.where(dx == 2, 12, 10))
        return jnp.where(dy == 0, same, other)

    def b_slot_time(m, q):
        d = (m - z + Z) % Z
        near = jnp.minimum(d, Z - d)
        turn = jnp.where(d < 4, PIECES - 1 - q, q)
        last = jnp.where((q == 1) | (q == 2), Z_STREAM - 1, Z_STREAM - 2)
        return jnp.where(near == 0, 0, jnp.where(near == 4, last, 4 * near - 4 + turn))

    def x_step(slot):
        for u, at in enumerate((0, 1, 2, 3, 4, 5, 7, 8, 9, 10, 11, 12)):
            @pl.when(slot == at)
            def _():
                x_copy(True, u, False).wait_recv()
                x_copy(False, u, False).wait_recv()
                if u > 0:
                    x_copy(True, u - 1, True).wait_send()
                    x_copy(False, u - 1, True).wait_send()

        for v, at in enumerate((4, 5, 6, 8)):
            @pl.when(slot == at)
            def _():
                y_copy(v, False).wait_recv()
                y_copy(v, True).wait_send()

        for u, at in ((3, 0), (4, 2), (5, 3), (6, 4), (7, 5), (8, 6), (9, 8), (10, 9), (11, 10)):
            @pl.when(slot == at)
            def _():
                x_send(jnp.int32(u))

    def slot_body(slot, _):
        z_copy(True, slot, False).wait_recv()
        z_copy(False, slot, False).wait_recv()

        @pl.when(slot == 9)
        def _():
            for d in range(1, 8):
                count_to_col(d).start()

        @pl.when(slot < Z_STREAM - 1 - DEPTH)
        def _():
            z_send(slot + DEPTH)

        @pl.when(slot == Z_STREAM - 1 - DEPTH)
        def _():
            for part in range(3):
                z_last(True, part, True).start()
                z_last(False, part, True).start()

            z_last(False, 3, True).start()

            @pl.when(z < Z - 1)
            def _():
                z_last(True, 3, True).start()

        @pl.when((slot == 10) & (z == 1))
        def _():
            z_last(False, 4, True).start()

        for place in (1, 2, 3):

            @pl.when((slot == 5 + place) & (z == place))
            def _():
                pl.semaphore_wait(last_in, 1)
                if place < 3:
                    signal(last_in, row=z_right)

        @pl.when(slot >= 2)
        def _():
            z_copy(True, slot - 2, True).wait_send()
            z_copy(False, slot - 2, True).wait_send()

        x_step(slot)

        @pl.when(slot == 5)
        def _():
            for d in range(1, 8):
                count_to_row(d).start()

        @pl.when(slot == 8)
        def _():
            for d in range(1, 8):
                count_to_row(d).wait_recv()
                count_to_row(d).wait_send()
            sum_cnt[...] = own_cnt[...] + jnp.sum(row_cnt[...], axis=0)

        def one_source(m, _):
            a_at = a_slot_time(m)

            def one_piece(q, _):
                @pl.when(jnp.maximum(a_at, b_slot_time(m, q)) == slot)
                def _():
                    multiply(m, (q,))

                return 0

            @pl.when(a_at <= slot)
            def _():
                lax.fori_loop(0, PIECES, one_piece, 0)

            return 0

        lax.fori_loop(0, Z, one_source, 0)
        return 0

    lax.fori_loop(0, Z_STREAM - 1, slot_body, 0)

    for d in range(1, 8):
        count_to_col(d).wait_recv()
        count_to_col(d).wait_send()
    everyone = sum_cnt[...] + jnp.sum(col_cnt[...], axis=0)
    tot_out[0] = everyone[0, 0]

    across = (z + 4) % Z
    for part in range(4):
        if part < 3:
            z_last(True, part, False).wait_recv()
        else:

            @pl.when(z > 0)
            def _():
                z_last(True, 3, False).wait_recv()

            @pl.when(z == 0)
            def _():
                z_last(False, 4, False).wait_recv()

        z_last(False, part, False).wait_recv()
    multiply(across, (1, 2))

    for right in (True, False):
        for t in (Z_STREAM - 3, Z_STREAM - 2):
            z_copy(right, t, True).wait_send()
        for part in range(3):
            z_last(right, part, True).wait_send()
        x_copy(right, X_STREAM - 1, True).wait_send()
    z_last(False, 3, True).wait_send()

    @pl.when(z < Z - 1)
    def _():
        z_last(True, 3, True).wait_send()

    @pl.when(z == 1)
    def _():
        z_last(False, 4, True).wait_send()


def round_kernel(acc, cnt, tot, out, cnt_out, tot_out, stage, sems):
    copies = [
        pltpu.make_async_copy(cnt, cnt_out, sems.at[4]),
        pltpu.make_async_copy(tot, tot_out, sems.at[5]),
    ]
    for copy in copies:
        copy.start()
    for i in range(4):
        rows = pl.ds(i * BLK, BLK)
        stage[:, i * BLK : (i + 1) * BLK, :] = acc[:, i * BLK : (i + 1) * BLK, :].astype(
            jnp.bfloat16
        )
        copy = pltpu.make_async_copy(stage.at[:, rows, :], out.at[:, rows, :], sems.at[i])
        copy.start()
        copies.append(copy)
    for copy in copies:
        copy.wait()


def shards(a_matrix, b_matrix, a_level, b_level, limit):
    parts, rows, columns = a_matrix.shape
    dma = pltpu.SemaphoreType.DMA
    smem = pl.BlockSpec(memory_space=pltpu.SMEM)
    hbm = pl.BlockSpec(memory_space=pltpu.HBM)
    acc, cnt, tot = pl.pallas_call(
        kernel,
        out_shape=(
            pltpu.VMEM((parts, rows, columns), jnp.float32),
            pltpu.SMEM((4, 4), jnp.int32),
            pltpu.SMEM((1,), jnp.int32),
        ),
        in_specs=[hbm] * 5,
        out_specs=(pl.BlockSpec(memory_space=pltpu.VMEM), smem, smem),
        scratch_shapes=[
            pltpu.SMEM((32, 32), jnp.int32),
            pltpu.SMEM((32, 32), jnp.int32),
            pltpu.SMEM((4, 4), jnp.int32),
            pltpu.VMEM((8, parts, rows, columns), jnp.bfloat16),
            pltpu.VMEM((Z, parts, rows, columns), jnp.bfloat16),
            pltpu.SMEM((32, 16), jnp.float32),
            pltpu.SMEM((33,), jnp.float32),
            pltpu.VMEM((1, BLK), jnp.int32),
            pltpu.VMEM((7, 1, BLK), jnp.int32),
            pltpu.VMEM((1, BLK), jnp.int32),
            pltpu.VMEM((7, 1, BLK), jnp.int32),
            dma((3,)),
            dma((2 * PIECES,)),
            dma((Z_STREAM + 4,)), dma((Z_STREAM + 4,)), dma((Z_STREAM + 4,)), dma((Z_STREAM + 4,)),
            dma((X_STREAM,)), dma((X_STREAM,)), dma((X_STREAM,)), dma((X_STREAM,)),
            dma((PIECES,)), dma((PIECES,)),
            dma((7,)), dma((7,)), dma((7,)), dma((7,)),
        ] + [pltpu.SemaphoreType.REGULAR] * 6,
        compiler_params=pltpu.CompilerParams(
            collective_id=0, has_side_effects=True, vmem_limit_bytes=61 << 20
        ),
        cost_estimate=pl.CostEstimate(
            flops=8 * rows * 4096 * columns, bytes_accessed=6 << 20, transcendentals=0
        ),
    )(a_level, b_level, limit, a_matrix, b_matrix)
    vmem = pl.BlockSpec(memory_space=pltpu.VMEM)
    return pl.pallas_call(
        round_kernel,
        out_shape=(
            jax.ShapeDtypeStruct((parts, rows, columns), jnp.bfloat16),
            jax.ShapeDtypeStruct((4, 4), jnp.int32),
            jax.ShapeDtypeStruct((1,), jnp.int32),
        ),
        in_specs=[vmem, smem, smem],
        out_specs=(hbm, hbm, hbm),
        scratch_shapes=[pltpu.VMEM((parts, rows, columns), jnp.bfloat16), dma((6,))],
        compiler_params=pltpu.CompilerParams(vmem_limit_bytes=48 << 20),
    )(acc, cnt, tot)


def solution(mesh):
    placed = (
        P("kpt", "row", "col"),
        P("kpt", "row", "col"),
        P("kpt", None),
        P("kpt", None),
        P(("kpt", "row"), "col"),
    )
    return jax.shard_map(
        shards,
        mesh=mesh,
        in_specs=placed,
        out_specs=(P("kpt", "row", "col"), P(("kpt", "row"), "col"), P("kpt")),
        check_vma=False,
    )
```

time: 94.2 us -> 89.8 us (0.953); the launches traced: 92.7 us -> 89.7 us
  Pallas kernels: 92.1 us -> 89.1 us
    pallas_call x1, Pallas kernels: 90.5 us -> 88 us  [shards(): pl.pallas_call(kernel, out_shape=(pltpu.VMEM((parts, rows, columns), jnp....]
where the time goes in v3:
time: 89.8 us; the launch traced here: 89.7 us
  Pallas kernels  89.1 us (99%)
    pallas_call x1, Pallas kernels, shards(): pl.pallas_call(kernel, out_shape=(pltpu.VMEM((parts, rows, columns), jnp....  88 us

profile of v3, /device:TPU:28, one launch (start us, length us, event | category | flops | bytes accessed | tf_op | source)
XLA Modules:
  0.0 89.7 jit_solution(18407915825023100652)
XLA Ops:
  0.6 88.0 %shard_map.76 = (f32[2,512,512]{2,1,0:T(8,128)S(1)}, s32[4,4]{1,0:T(4,128)S(4)}, s32[1]{0:T(128)S(4)}) custom-call(s32[32,32]{1,0:T(8,128)} %a_lev_hbm.1, s32[32,32]{1,0:T(8,128)} %b_lev_hbm.1, s32[4,4]{1,0:T(4,128)} %lim_hbm.1, bf16[2,512,512]{2,1,0:T(8,128)(2,1)} %a_hbm.1, bf16[2,512,512]{2,1,0:T(8,128)(2,1)} %b_hbm.1), custom_call_target="tpu_custom_call" | custom-call | flops 8589934592 | bytes 6291456 | tf_op jit(solution)/shard_map/pallas_call | solution.py:478
  88.7 1.0 %shard_map.77 = (bf16[2,512,512]{2,1,0:T(8,128)(2,1)}, s32[4,4]{1,0:T(4,128)}, s32[1]{0:T(128)}) custom-call(f32[2,512,512]{2,1,0:T(8,128)S(1)} %get-tuple-element.6.acc, s32[4,4]{1,0:T(4,128)S(4)} %get-tuple-element.7.cnt, s32[1]{0:T(128)S(4)} %get-tuple-element.8.tot), custom_call_target="tpu_custom_call" | custom-call | tf_op jit(solution)/shard_map/pallas_call | solution.py:514

commit v4 on v3

--- a/solution.py
+++ b/solution.py
@@ -15,6 +15,7 @@
 X_STREAM = 12
 DEPTH = 4
 X_DEPTH = 3
+SHIFT = 48
 MESH = pl.DeviceIdType.MESH
 
 
@@ -51,7 +52,9 @@
         a_in.append(
             pltpu.make_async_copy(a_hbm.at[:, rows, :], piece(a_buf, c, q), in_sem.at[PIECES + q])
         )
+    for q in (0, 3, 1, 2):
         b_in[q].start()
+    for q in range(PIECES):
         a_in[q].start()
     levels_in = [
         pltpu.make_async_copy(there, here, lev_sem.at[n])
@@ -116,14 +119,15 @@
         )
 
     def z_last(right, part, sending):
-        q = 1 if right or part == 4 else 2
+        q = 1 if right or part == 1 else 2
         far = 3 if sending else 4
         origin = (z - far + Z) % Z if right else (z + far) % Z
         sems = (zr_send, zr_recv) if right else (zl_send, zl_recv)
-        quarter = 3 if part == 4 else part
-        block = b_buf.at[origin, :, pl.ds(q * BLK, BLK), pl.ds(quarter * BLK, BLK)]
+        begin = BLK - SHIFT if part == 1 else 0
+        end = BLK - SHIFT if right and part == 0 else BLK
+        rows = b_buf.at[origin, :, pl.ds(q * BLK + begin, end - begin), :]
         return pltpu.make_async_remote_copy(
-            block, block, sems[0].at[Z_STREAM - 1 + part], sems[1].at[Z_STREAM - 1 + part],
+            rows, rows, sems[0].at[Z_STREAM - 1 + part], sems[1].at[Z_STREAM - 1 + part],
             device_id={"row": z_right if right else z_left}, device_id_type=MESH,
         )
 
@@ -180,30 +184,41 @@
         for q in range(X_DEPTH):
             x_copy(right, jnp.int32(q), True).start()
 
-    for q in range(DEPTH):
+    @pl.when(z == Z - 1)
+    def _():
+        signal(from_left, row=z_right)
+
+    @pl.when(z > 0)
+    def _():
+        signal(from_right, row=z_left)
+
+    @pl.when(x == X - 1)
+    def _():
+        signal(from_x_left, col=x_right)
+
+    @pl.when(x > 0)
+    def _():
+        signal(from_x_right, col=x_left)
+
+    @pl.when(yh == 1)
+    def _():
+        signal(from_y, col=y_far)
+
+    for q, to_right, to_left in ((0, (0,), ()), (3, (), (0,)), (1, (1,), ()), (2, (2, 3), (1, 2, 3))):
         b_in[q].wait()
-
-    @pl.when(z == Z - 1)
-    def _():
-        first_z(True)
-        signal(from_left, row=z_right)
-
-    @pl.when(z > 0)
-    def _():
-        first_z(False)
-        signal(from_right, row=z_left)
-
-    @pl.when(x == X - 1)
-    def _():
-        signal(from_x_left, col=x_right)
-
-    @pl.when(x > 0)
-    def _():
-        signal(from_x_right, col=x_left)
-
-    @pl.when(yh == 1)
-    def _():
-        signal(from_y, col=y_far)
+        if to_right:
+
+            @pl.when(z == Z - 1)
+            def _():
+                for t in to_right:
+                    z_copy(True, jnp.int32(t), True).start()
+
+        if to_left:
+
+            @pl.when(z > 0)
+            def _():
+                for t in to_left:
+                    z_copy(False, jnp.int32(t), True).start()
 
     @pl.when(z < Z - 1)
     def _():
@@ -349,19 +364,16 @@
 
         @pl.when(slot == Z_STREAM - 1 - DEPTH)
         def _():
-            for part in range(3):
-                z_last(True, part, True).start()
-                z_last(False, part, True).start()
-
-            z_last(False, 3, True).start()
+            z_last(True, 0, True).start()
+            z_last(False, 0, True).start()
 
             @pl.when(z < Z - 1)
             def _():
-                z_last(True, 3, True).start()
+                z_last(True, 1, True).start()
 
         @pl.when((slot == 10) & (z == 1))
         def _():
-            z_last(False, 4, True).start()
+            z_last(False, 1, True).start()
 
         for place in (1, 2, 3):
 
@@ -418,37 +430,32 @@
     tot_out[0] = everyone[0, 0]
 
     across = (z + 4) % Z
-    for part in range(4):
-        if part < 3:
-            z_last(True, part, False).wait_recv()
-        else:
-
-            @pl.when(z > 0)
-            def _():
-                z_last(True, 3, False).wait_recv()
-
-            @pl.when(z == 0)
-            def _():
-                z_last(False, 4, False).wait_recv()
-
-        z_last(False, part, False).wait_recv()
+    z_last(True, 0, False).wait_recv()
+    z_last(False, 0, False).wait_recv()
+
+    @pl.when(z > 0)
+    def _():
+        z_last(True, 1, False).wait_recv()
+
+    @pl.when(z == 0)
+    def _():
+        z_last(False, 1, False).wait_recv()
+
     multiply(across, (1, 2))
 
     for right in (True, False):
         for t in (Z_STREAM - 3, Z_STREAM - 2):
             z_copy(right, t, True).wait_send()
-        for part in range(3):
-            z_last(right, part, True).wait_send()
+        z_last(right, 0, True).wait_send()
         x_copy(right, X_STREAM - 1, True).wait_send()
-    z_last(False, 3, True).wait_send()
 
     @pl.when(z < Z - 1)
     def _():
-        z_last(True, 3, True).wait_send()
+        z_last(True, 1, True).wait_send()
 
     @pl.when(z == 1)
     def _():
-        z_last(False, 4, True).wait_send()
+        z_last(False, 1, True).wait_send()
 
 
 def round_kernel(acc, cnt, tot, out, cnt_out, tot_out, stage, sems):
@@ -498,7 +505,7 @@
             pltpu.VMEM((7, 1, BLK), jnp.int32),
             dma((3,)),
             dma((2 * PIECES,)),
-            dma((Z_STREAM + 4,)), dma((Z_STREAM + 4,)), dma((Z_STREAM + 4,)), dma((Z_STREAM + 4,)),
+            dma((Z_STREAM + 1,)), dma((Z_STREAM + 1,)), dma((Z_STREAM + 1,)), dma((Z_STREAM + 1,)),
             dma((X_STREAM,)), dma((X_STREAM,)), dma((X_STREAM,)), dma((X_STREAM,)),
             dma((PIECES,)), dma((PIECES,)),
             dma((7,)), dma((7,)), dma((7,)), dma((7,)),

time: 89.8 us -> 89.6 us (level)
  no operation moved by 1% of the time
where the time goes in v4:
time: 89.6 us; the launch traced here: 89.4 us
  Pallas kernels  88.8 us (99%)
    pallas_call x1, Pallas kernels, shards(): pl.pallas_call(kernel, out_shape=(pltpu.VMEM((parts, rows, columns), jnp....  87.8 us

profile of v4, /device:TPU:28, one launch (start us, length us, event | category | flops | bytes accessed | tf_op | source)
XLA Modules:
  0.0 89.4 jit_solution(14509353960814114127)
XLA Ops:
  0.6 87.8 %shard_map.76 = (f32[2,512,512]{2,1,0:T(8,128)S(1)}, s32[4,4]{1,0:T(4,128)S(4)}, s32[1]{0:T(128)S(4)}) custom-call(s32[32,32]{1,0:T(8,128)} %a_lev_hbm.1, s32[32,32]{1,0:T(8,128)} %b_lev_hbm.1, s32[4,4]{1,0:T(4,128)} %lim_hbm.1, bf16[2,512,512]{2,1,0:T(8,128)(2,1)} %a_hbm.1, bf16[2,512,512]{2,1,0:T(8,128)(2,1)} %b_hbm.1), custom_call_target="tpu_custom_call" | custom-call | flops 8589934592 | bytes 6291456 | tf_op jit(solution)/shard_map/pallas_call | solution.py:485
  88.4 1.0 %shard_map.77 = (bf16[2,512,512]{2,1,0:T(8,128)(2,1)}, s32[4,4]{1,0:T(4,128)}, s32[1]{0:T(128)}) custom-call(f32[2,512,512]{2,1,0:T(8,128)S(1)} %get-tuple-element.6.acc, s32[4,4]{1,0:T(4,128)S(4)} %get-tuple-element.7.cnt, s32[1]{0:T(128)S(4)} %get-tuple-element.8.tot), custom_call_target="tpu_custom_call" | custom-call | tf_op jit(solution)/shard_map/pallas_call | solution.py:521

commit v5 on v4

--- a/solution.py
+++ b/solution.py
@@ -460,14 +460,15 @@
 
 def round_kernel(acc, cnt, tot, out, cnt_out, tot_out, stage, sems):
     copies = [
-        pltpu.make_async_copy(cnt, cnt_out, sems.at[4]),
-        pltpu.make_async_copy(tot, tot_out, sems.at[5]),
+        pltpu.make_async_copy(cnt, cnt_out, sems.at[8]),
+        pltpu.make_async_copy(tot, tot_out, sems.at[9]),
     ]
     for copy in copies:
         copy.start()
-    for i in range(4):
-        rows = pl.ds(i * BLK, BLK)
-        stage[:, i * BLK : (i + 1) * BLK, :] = acc[:, i * BLK : (i + 1) * BLK, :].astype(
+    half = BLK // 2
+    for i in range(8):
+        rows = pl.ds(i * half, half)
+        stage[:, i * half : (i + 1) * half, :] = acc[:, i * half : (i + 1) * half, :].astype(
             jnp.bfloat16
         )
         copy = pltpu.make_async_copy(stage.at[:, rows, :], out.at[:, rows, :], sems.at[i])
@@ -527,7 +528,7 @@
         ),
         in_specs=[vmem, smem, smem],
         out_specs=(hbm, hbm, hbm),
-        scratch_shapes=[pltpu.VMEM((parts, rows, columns), jnp.bfloat16), dma((6,))],
+        scratch_shapes=[pltpu.VMEM((parts, rows, columns), jnp.bfloat16), dma((10,))],
         compiler_params=pltpu.CompilerParams(vmem_limit_bytes=48 << 20),
     )(acc, cnt, tot)
 

time: 89.6 us -> 89.6 us (level)
  no operation moved by 1% of the time
where the time goes in v5:
time: 89.6 us; the launch traced here: 89.5 us
  Pallas kernels  88.8 us (99%)
    pallas_call x1, Pallas kernels, shards(): pl.pallas_call(kernel, out_shape=(pltpu.VMEM((parts, rows, columns), jnp....  87.8 us

profile of v5, /device:TPU:28, one launch (start us, length us, event | category | flops | bytes accessed | tf_op | source)
XLA Modules:
  0.0 89.5 jit_solution(5887518383799342727)
XLA Ops:
  0.6 87.8 %shard_map.76 = (f32[2,512,512]{2,1,0:T(8,128)S(1)}, s32[4,4]{1,0:T(4,128)S(4)}, s32[1]{0:T(128)S(4)}) custom-call(s32[32,32]{1,0:T(8,128)} %a_lev_hbm.1, s32[32,32]{1,0:T(8,128)} %b_lev_hbm.1, s32[4,4]{1,0:T(4,128)} %lim_hbm.1, bf16[2,512,512]{2,1,0:T(8,128)(2,1)} %a_hbm.1, bf16[2,512,512]{2,1,0:T(8,128)(2,1)} %b_hbm.1), custom_call_target="tpu_custom_call" | custom-call | flops 8589934592 | bytes 6291456 | tf_op jit(solution)/shard_map/pallas_call | solution.py:486
  88.4 1.1 %shard_map.77 = (bf16[2,512,512]{2,1,0:T(8,128)(2,1)}, s32[4,4]{1,0:T(4,128)}, s32[1]{0:T(128)}) custom-call(f32[2,512,512]{2,1,0:T(8,128)S(1)} %get-tuple-element.6.acc, s32[4,4]{1,0:T(4,128)S(4)} %get-tuple-element.7.cnt, s32[1]{0:T(128)S(4)} %get-tuple-element.8.tot), custom_call_target="tpu_custom_call" | custom-call | tf_op jit(solution)/shard_map/pallas_call | solution.py:522
